TPU v7x, 32 devices: a whole 2x2x4 slice. The times are simulated.
32 devices in a mesh: sweep: 1, dp: 8 (over z, y), tensor: 4 (over x, core).
Axes of the slice: x: 2, y: 2, z: 4, core: 2. Of those that a mesh axis runs over, the one named last changes fastest.
Arguments:
- checkpoint: bfloat16 [1024, 8192], P(('sweep', 'dp'), 'tensor'), may hold values from -6 to 6
- norm_gain: bfloat16 [8192], P(('sweep', 'tensor')), may hold values from 0.5 to 1.5
- w_query: bfloat16 [8192, 4096], P(('sweep', 'dp'), 'tensor'), may hold values from -1 to 1
- w_key: bfloat16 [8192, 512], P(('sweep', 'dp'), 'tensor'), may hold values from -8 to 8
- w_value: bfloat16 [8192, 512], P(('sweep', 'dp'), 'tensor'), may hold values from -0.0625 to 0.0625
- grad_attn: bfloat16 [1024, 4096], P(('sweep', 'dp'), 'tensor'), may hold values from -6 to 6
Outputs:
- d_checkpoint: bfloat16 [1024, 8192], P(('sweep', 'dp'), 'tensor')
- grad_gain: float32 [8192], P(('sweep', 'tensor'))
- grad_query: float32 [8192, 4096], P(('sweep', 'dp'), 'tensor')
- grad_key: float32 [8192, 512], P(('sweep', 'dp'), 'tensor')
- grad_value: float32 [8192, 512], P(('sweep', 'dp'), 'tensor')
All inputs are finite; a program needn't handle non-finite values.
Results may differ from a plain program's by a relative error of at most 0.025.
The roundings to bfloat16 on the way count: a program that leaves them out, or rounds other values in their place, can miss the bound.
Values may be sent and summed in bfloat16 or wider, within the bound.
No kernel may reach another device: no remote copies, remote signals or barrier semaphores. Data moves between devices by JAX's collectives and lax.ppermute only.
A program may use at most 128 MiB of HBM per device.

v0:
```python
import jax
import jax.numpy as jnp
from jax import lax
from jax.sharding import PartitionSpec as P

QHEADS = 32
KVHEADS = 4
HD = 128


EPS = 1e-05
THETA = 500000.0


def round_half(field):
    return lax.optimization_barrier(field.astype(jnp.bfloat16))


def angles(positions, head_width):
    frequency = THETA ** (-(jnp.arange(head_width // 2, dtype=jnp.float32) * 2.0) / head_width)
    turned = positions.astype(jnp.float32)[:, None] * frequency[None, :]
    return (jnp.cos(turned)[:, None, :], jnp.sin(turned)[:, None, :])


def rotate(field, cosine_table, sine_table):
    half_width = field.shape[-1] // 2
    front_half = field[..., :half_width]
    back_half = field[..., half_width:]
    return jnp.concatenate(
        [
            front_half * cosine_table - back_half * sine_table,
            back_half * cosine_table + front_half * sine_table,
        ],
        -1,
    )


def rotate_back(field, cosine_table, sine_table):
    half_width = field.shape[-1] // 2
    front_half = field[..., :half_width]
    back_half = field[..., half_width:]
    return jnp.concatenate(
        [
            front_half * cosine_table + back_half * sine_table,
            back_half * cosine_table - front_half * sine_table,
        ],
        -1,
    )


def project_back(grads, matrix):
    return jnp.einsum("tc,dc->td", grads, matrix, preferred_element_type=jnp.float32)


def on_device(checkpoint, norm_gain, w_query, w_key, w_value, grad_attn):
    row_count = checkpoint.shape[0]
    head_width = HD
    group_size = QHEADS // KVHEADS
    full_x, full_gain = (
        lax.all_gather(checkpoint, "tensor", axis=1, tiled=True),
        lax.all_gather(norm_gain, "tensor", axis=0, tiled=True),
    )
    x_wide = full_x.astype(jnp.float32)
    gain_wide = full_gain.astype(jnp.float32)
    model_width = full_x.shape[1]
    inverse = lax.rsqrt(jnp.mean(x_wide * x_wide, -1, keepdims=True) + EPS)
    normed = (x_wide * inverse * gain_wide).astype(jnp.bfloat16)
    query_all, key_all, value_all = (
        lax.all_gather(w_query, "dp", axis=0, tiled=True),
        lax.all_gather(w_key, "dp", axis=0, tiled=True),
        lax.all_gather(w_value, "dp", axis=0, tiled=True),
    )
    q_heads = query_all.shape[1] // head_width
    own_kv = max(1, q_heads // group_size)
    run_heads = q_heads // own_kv
    first_kv = lax.axis_index("tensor") * q_heads // group_size
    queries = jnp.dot(normed, query_all, preferred_element_type=jnp.float32).reshape(
        row_count, q_heads, head_width
    )
    key_local = jnp.dot(normed, key_all, preferred_element_type=jnp.float32)
    value_local = jnp.dot(normed, value_all, preferred_element_type=jnp.float32)
    key_cols_all, value_cols_all = (
        lax.all_gather(key_local, "tensor", axis=1, tiled=True),
        lax.all_gather(value_local, "tensor", axis=1, tiled=True),
    )
    kv_total = key_cols_all.shape[1] // head_width
    first_row = lax.axis_index("dp") * row_count
    own_positions = first_row + jnp.arange(row_count, dtype=jnp.int32)
    cosine_table, sine_table = angles(own_positions, head_width)
    query_rot = rotate(queries, cosine_table, sine_table).astype(jnp.bfloat16)
    key_heads = lax.dynamic_slice_in_dim(
        key_cols_all.reshape(row_count, head_width, kv_total), first_kv, own_kv, 2
    )
    value_heads = lax.dynamic_slice_in_dim(
        value_cols_all.reshape(row_count, head_width, kv_total), first_kv, own_kv, 2
    )
    key_turned = rotate(jnp.transpose(key_heads, (0, 2, 1)), cosine_table, sine_table)
    key_rot = key_turned.astype(jnp.bfloat16).reshape(row_count, own_kv * head_width)
    value_half = (
        jnp.transpose(value_heads, (0, 2, 1))
        .astype(jnp.bfloat16)
        .reshape(row_count, own_kv * head_width)
    )
    gathered_keys, gathered_values = (
        lax.all_gather(key_rot, "dp", axis=0, tiled=True),
        lax.all_gather(value_half, "dp", axis=0, tiled=True),
    )
    seq_length = gathered_keys.shape[0]
    keys_three = gathered_keys.reshape(seq_length, own_kv, head_width)
    values_three = gathered_values.reshape(seq_length, own_kv, head_width)
    score_scale = head_width ** (-0.5)
    query_grp = query_rot.reshape(row_count, own_kv, run_heads, head_width)
    upstream = grad_attn.reshape(row_count, own_kv, run_heads, head_width)
    scores = (
        jnp.einsum("tkgd,skd->kgts", query_grp, keys_three, preferred_element_type=jnp.float32)
        * score_scale
    )
    allowed = own_positions[:, None] >= jnp.arange(seq_length, dtype=jnp.int32)[None, :]
    scores = jnp.where(allowed, scores, -jnp.inf)
    row_top = jnp.max(scores, -1, keepdims=True)
    raw_weights = jnp.exp(scores - row_top)
    chances = raw_weights / jnp.sum(raw_weights, -1, keepdims=True)
    chances_half = chances.astype(jnp.bfloat16)
    attended = jnp.einsum(
        "kgts,skd->tkgd", chances_half, values_three, preferred_element_type=jnp.float32
    )
    row_delta = jnp.sum(upstream.astype(jnp.float32) * attended, -1)
    prob_grads = jnp.einsum(
        "tkgd,skd->kgts", upstream, values_three, preferred_element_type=jnp.float32
    )
    dscore = chances * (prob_grads - jnp.transpose(row_delta, (1, 2, 0))[..., None])
    dscore_half = dscore.astype(jnp.bfloat16)
    dquery = (
        jnp.einsum("kgts,skd->tkgd", dscore_half, keys_three, preferred_element_type=jnp.float32)
        * score_scale
    )
    dkey_part = (
        jnp.einsum("kgts,tkgd->skd", dscore_half, query_grp, preferred_element_type=jnp.float32)
        * score_scale
    )
    dvalue_part = jnp.einsum(
        "kgts,tkgd->skd", chances_half, upstream, preferred_element_type=jnp.float32
    )
    dkey_sum, dvalue_sum = (
        lax.psum_scatter(
            dkey_part.reshape(seq_length, own_kv * head_width).astype(jnp.bfloat16),
            "dp",
            scatter_dimension=0,
            tiled=True,
        ).astype(jnp.float32),
        lax.psum_scatter(
            dvalue_part.reshape(seq_length, own_kv * head_width).astype(jnp.bfloat16),
            "dp",
            scatter_dimension=0,
            tiled=True,
        ).astype(jnp.float32),
    )
    dkey_back = rotate_back(
        dkey_sum.reshape(row_count, own_kv, head_width), cosine_table, sine_table
    )
    dvalue_back = dvalue_sum.reshape(row_count, own_kv, head_width)
    empty_heads = jnp.zeros((row_count, kv_total, head_width), jnp.float32)
    zero_start = jnp.zeros((), jnp.int32)
    dkey_embed = lax.dynamic_update_slice(
        empty_heads, dkey_back, (zero_start, first_kv, zero_start)
    )
    dvalue_embed = lax.dynamic_update_slice(
        empty_heads, dvalue_back, (zero_start, first_kv, zero_start)
    )
    dkey_embed = jnp.transpose(dkey_embed, (0, 2, 1)).reshape(row_count, head_width * kv_total)
    dvalue_embed = jnp.transpose(dvalue_embed, (0, 2, 1)).reshape(row_count, head_width * kv_total)
    dkey_cols, dvalue_cols = (
        lax.psum_scatter(
            dkey_embed.astype(jnp.bfloat16), "tensor", scatter_dimension=1, tiled=True
        ).astype(jnp.float32),
        lax.psum_scatter(
            dvalue_embed.astype(jnp.bfloat16), "tensor", scatter_dimension=1, tiled=True
        ).astype(jnp.float32),
    )
    dquery_pre = (
        rotate_back(dquery.reshape(row_count, q_heads, head_width), cosine_table, sine_table)
        .astype(jnp.bfloat16)
        .reshape(row_count, q_heads * head_width)
    )
    dkey_pre = dkey_cols.astype(jnp.bfloat16)
    dvalue_pre = dvalue_cols.astype(jnp.bfloat16)
    partial_input = (
        project_back(dquery_pre, query_all)
        + project_back(dkey_pre, key_all)
        + project_back(dvalue_pre, value_all)
    )
    slice_width = checkpoint.shape[1]
    x_own = checkpoint.astype(jnp.float32)
    gain_own = norm_gain.astype(jnp.float32)
    input_full = lax.psum(partial_input.astype(jnp.bfloat16), "tensor").astype(jnp.float32)
    row_sum = jnp.sum(gain_wide * input_full * x_wide, -1, keepdims=True)
    input_own = lax.dynamic_slice_in_dim(
        input_full, lax.axis_index("tensor") * slice_width, slice_width, 1
    )
    d_checkpoint = (
        inverse * gain_own * input_own - x_own * inverse**3 * row_sum / model_width
    ).astype(jnp.bfloat16)
    grad_gain = lax.psum(jnp.sum(input_own * x_own * inverse, 0), "dp")
    token_grads = jnp.concatenate([dquery_pre, dkey_pre, dvalue_pre], 1)
    own_rows = w_query.shape[0]
    feature_cols = lax.all_to_all(normed, "dp", split_axis=1, concat_axis=0, tiled=True)
    piece = lax.all_gather(token_grads, "dp", axis=0, tiled=True)
    piece_rows = piece.shape[0]
    blocks = piece_rows // row_count
    block_x = feature_cols.reshape(blocks, row_count, own_rows)
    block_g = piece.reshape(blocks, row_count, piece.shape[1])
    terms = jnp.einsum("btd,btc->bdc", block_x, block_g, preferred_element_type=jnp.float32)
    weight_grads = jnp.sum(round_half(terms).astype(jnp.float32), 0)
    query_cols = w_query.shape[1]
    key_cols = w_key.shape[1]
    grad_query = weight_grads[:, :query_cols]
    grad_key = weight_grads[:, query_cols : query_cols + key_cols]
    grad_value = weight_grads[:, query_cols + key_cols :]
    return (d_checkpoint, grad_gain, grad_query, grad_key, grad_value)


def solution(mesh):
    return jax.shard_map(
        on_device,
        mesh=mesh,
        in_specs=(
            P(("sweep", "dp"), "tensor"),
            P(("sweep", "tensor")),
            P(("sweep", "dp"), "tensor"),
            P(("sweep", "dp"), "tensor"),
            P(("sweep", "dp"), "tensor"),
            P(("sweep", "dp"), "tensor"),
        ),
        out_specs=(
            P(("sweep", "dp"), "tensor"),
            P(("sweep", "tensor")),
            P(("sweep", "dp"), "tensor"),
            P(("sweep", "dp"), "tensor"),
            P(("sweep", "dp"), "tensor"),
        ),
        check_vma=False,
    )
```

profile of v0, /device:TPU:0, one launch (start us, length us, event | category | flops | bytes accessed | tf_op | source)
XLA Modules:
  0.0 710.5 jit_solution(5812037475579603408)
XLA Ops:
  10.0 6.4 all_gather.31
  18.0 16.9 %all-gather.7.cloned.1.call-done = bf16[128,8192]{1,0:T(8,128)(2,1)} async-done(((bf16[128,2048]{1,0:T(8,128)(2,1)}), bf16[128,8192]{1,0:T(8,128)(2,1)}) %all-gather.7.cloned.1.call-update) | async-done | bytes 2097168 | tf_op jit(solution)/shard_map/all_gather | solution.py:60
  36.9 2.2 fusion.3
  39.1 47.0 %all-gather.13.cloned.1.call-done = bf16[8192,128]{1,0:T(8,128)(2,1)} async-done(((bf16[1024,128]{1,0:T(8,128)(2,1)}), bf16[8192,128]{1,0:T(8,128)(2,1)}) %all-gather.13.cloned.1.call-update) | async-done | bytes 2097168 | tf_op jit(solution)/shard_map/all_gather | solution.py:71
  86.1 2.3 fusion.90
  88.4 5.4 all_gather.37
  94.2 41.7 %all-gather.9.cloned.1.call-done = bf16[8192,128]{1,0:T(8,128)(2,1)} async-done(((bf16[1024,128]{1,0:T(8,128)(2,1)}), bf16[8192,128]{1,0:T(8,128)(2,1)}) %all-gather.9.cloned.1.call-update) | async-done | bytes 2097168 | tf_op jit(solution)/shard_map/all_gather | solution.py:70
  135.9 2.3 fusion.89
  138.2 5.8 all_gather.33
  144.7 32.5 %all_gather.34 = bf16[1024,128]{1,0:T(8,128)(2,1)S(1)} all-gather(bf16[128,128]{1,0:T(8,128)(2,1)S(1)} %pad_maximum_fusion.6), channel_id=1, replica_groups=mesh['sweep'=1,'dp'=8,'tensor'=4] {'dp'}, dimensions={0}, use_global_device_ids=true | all-gather | bytes 294912 | tf_op jit(solution)/shard_map/all_gather | solution.py:105
  177.2 34.9 %all-gather = bf16[1024,128,1]{1,0,2:T(8,128)(2,1)} all-gather(bf16[128,128,1]{1,0,2:T(8,128)(2,1)S(1)} %copy.84), channel_id=2, replica_groups=mesh['sweep'=1,'dp'=8,'tensor'=4] {'dp'}, dimensions={0}, use_global_device_ids=true | all-gather | bytes 294912 | tf_op jit(solution)/shard_map/all_gather | solution.py:106
  212.1 155.9 %all-gather.11.cloned.1.call-done = bf16[8192,1024]{1,0:T(8,128)(2,1)} async-done(((bf16[1024,1024]{1,0:T(8,128)(2,1)}), bf16[8192,1024]{1,0:T(8,128)(2,1)}) %all-gather.11.cloned.1.call-update) | async-done | bytes 16777232 | tf_op jit(solution)/shard_map/all_gather | solution.py:69
  368.0 8.1 %convolution_bitcast_fusion = f32[16,8,8,128]{3,1,2,0:T(8,128)S(1)} fusion(bf16[128,8192]{1,0:T(8,128)(2,1)S(1)} %fusion.3, bf16[8192,1024]{1,0:T(8,128)(2,1)} %all-gather.11.cloned.1.call-done), kind=kOutput, calls=%fused_computation.37 | convolution fusion | flops 2147483648 | bytes 19398656 | tf_op jit(solution)/shard_map/dot_general | solution.py:77
  383.9 2.5 fusion.32
  387.1 4.0 fusion.41
  391.2 56.3 %reduce-scatter.5.cloned.1.call-done = bf16[128,128]{1,0:T(8,128)(2,1)} async-done(((bf16[1024,128]{1,0:T(8,128)(2,1)}), bf16[128,128]{1,0:T(8,128)(2,1)}) %reduce-scatter.5.cloned.1.call-update) | async-done | bytes 32784 | tf_op jit(solution)/shard_map/reduce_scatter | solution.py:145
  451.3 13.5 %fusion.91 = f32[128,8192]{1,0:T(8,128)} fusion(bf16[128,1024]{0,1:T(8,128)(2,1)S(1)} %bitcast.168, bf16[8192,1024]{1,0:T(8,128)(2,1)} %all-gather.11.cloned.1.call-done), kind=kOutput, calls=%fused_computation.102 | convolution fusion | flops 2147483648 | bytes 21233664 | tf_op jit(solution)/shard_map/tc,dc->td/dot_general | solution.py:52
  464.8 47.7 %reduce-scatter.9.cloned.1.call-done = bf16[128,128]{1,0:T(8,128)(2,1)} async-done(((bf16[1024,128]{1,0:T(8,128)(2,1)}), bf16[128,128]{1,0:T(8,128)(2,1)}) %reduce-scatter.9.cloned.1.call-update) | async-done | bytes 32784 | tf_op jit(solution)/shard_map/reduce_scatter | solution.py:151
  515.6 18.7 %reduce-scatter.7.cloned.1.call-done = bf16[128,128]{0,1:T(8,128)(2,1)} async-done(((bf16[128,512]{0,1:T(8,128)(2,1)}), bf16[128,128]{0,1:T(8,128)(2,1)}) %reduce-scatter.7.cloned.1.call-update) | async-done | bytes 32784 | tf_op jit(solution)/shard_map/reduce_scatter | solution.py:173
  534.2 5.6 convolution_add_fusion.1
  539.8 17.1 %reduce-scatter.11.cloned.1.call-done = bf16[128,128]{0,1:T(8,128)(2,1)} async-done(((bf16[128,512]{0,1:T(8,128)(2,1)}), bf16[128,128]{0,1:T(8,128)(2,1)}) %reduce-scatter.11.cloned.1.call-update) | async-done | bytes 32784 | tf_op jit(solution)/shard_map/reduce_scatter | solution.py:176
  556.9 4.9 fusion
  562.7 2.4 copy.81
  565.2 5.5 all-to-all-start
  570.7 42.7 %all-reduce.2.cloned.1.call-done = bf16[128,8192]{1,0:T(8,128)(2,1)} async-done(((bf16[128,8192]{1,0:T(8,128)(2,1)}), bf16[128,8192]{1,0:T(8,128)(2,1)}) %all-reduce.2.cloned.1.call-update) | async-done | bytes 2097168 | tf_op jit(solution)/shard_map/psum | solution.py:195
  613.4 2.2 convert_element_type.142
  617.8 23.2 %psum.15 = f32[2048]{0:T(1024)} all-reduce(f32[2048]{0:T(1024)S(1)} %get-tuple-element.7), channel_id=1, replica_groups=mesh['sweep'=1,'dp'=8,'tensor'=4] {'dp'}, use_global_device_ids=true, to_apply=%region_11.12 | all-reduce | flops 2048 | bytes 16384 | tf_op jit(solution)/shard_map/psum | solution.py:203
  641.0 31.3 %all-gather.15.cloned.1.call-done = bf16[1024,1280]{0,1:T(8,128)(2,1)} async-done(((bf16[128,1280]{0,1:T(8,128)(2,1)}), bf16[1024,1280]{0,1:T(8,128)(2,1)}) %all-gather.15.cloned.1.call-update) | async-done | bytes 2621456 | tf_op jit(solution)/shard_map/all_gather | solution.py:207
  672.4 4.4 copy.69
  676.7 11.9 %convolution_convert_fusion = bf16[8,1024,1280]{2,1,0:T(8,128)(2,1)} fusion(bf16[8,128,1280]{2,1,0:T(8,128)(2,1)} %bitcast.165, bf16[128,8,1024]{0,2,1:T(8,128)(2,1)} %all-to-all-done), kind=kOutput, calls=%fused_computation.1 | convolution fusion | flops 2694840320 | bytes 25690112 | tf_op jit(solution)/shard_map/btd,btc->bdc/dot_general | solution.py:212
  688.7 11.3 %convert_reduce_fusion = f32[1024,1280]{1,0:T(8,128)S(1)} fusion(bf16[8,1024,1280]{2,1,0:T(8,128)(2,1)} %convolution_convert_fusion), kind=kLoop, calls=%fused_computation | loop fusion | flops 19660800 | bytes 26214400 | tf_op jit(solution)/shard_map/reduce_sum | solution.py:213
  701.0 2.7 slice.52
  (87 shorter events, 26.7 us)
Async XLA Ops:
  7.2 27.7 %all-gather.7.cloned.1.call-start = ((), (), s32[]{:S(2)}) async-start(), calls=%async_computation.5 | async-start | bytes 2621440 | tf_op jit(solution)/shard_map/all_gather | solution.py:60
  7.9 78.2 %all-gather.13.cloned.1.call-start = ((), (), s32[]{:S(2)}) async-start(), calls=%async_computation.8 | async-start | bytes 2359296 | tf_op jit(solution)/shard_map/all_gather | solution.py:71
  8.6 127.2 %all-gather.9.cloned.1.call-start = ((), (), s32[]{:S(2)}) async-start(), calls=%async_computation.6 | async-start | bytes 2359296 | tf_op jit(solution)/shard_map/all_gather | solution.py:70
  9.4 358.6 %all-gather.11.cloned.1.call-start = ((), (), s32[]{:S(2)}) async-start(), calls=%async_computation.7 | async-start | bytes 18874368 | tf_op jit(solution)/shard_map/all_gather | solution.py:69
  10.0 437.6 %reduce-scatter.5.cloned.1.call-start = ((), (), s32[]{:S(2)}) async-start(), calls=%async_computation.9 | async-start | bytes 294912 | tf_op jit(solution)/shard_map/reduce_scatter | solution.py:145
  376.6 1.7 copy-start.8
  377.4 2.2 copy-start.1
  378.3 1.3 copy-start.7
  381.1 1.3 copy-start.4
  387.1 125.4 %reduce-scatter.9.cloned.1.call-start = ((), (), s32[]{:S(2)}) async-start(), calls=%async_computation.11 | async-start | bytes 294912 | tf_op jit(solution)/shard_map/reduce_scatter | solution.py:151
  391.2 143.0 %reduce-scatter.7.cloned.1.call-start = ((), (), s32[]{:S(2)}) async-start(), calls=%async_computation.10 | async-start | bytes 163840 | tf_op jit(solution)/shard_map/reduce_scatter | solution.py:173
  450.3 0.7 copy-start.6
  451.0 105.9 %reduce-scatter.11.cloned.1.call-start = ((), (), s32[]{:S(2)}) async-start(), calls=%async_computation.12 | async-start | bytes 163840 | tf_op jit(solution)/shard_map/reduce_scatter | solution.py:176
  514.8 0.7 copy-start.5
  515.5 97.9 %all-reduce.2.cloned.1.call-start = ((), (), s32[]{:S(2)}) async-start(), calls=%async_computation.13 | async-start | bytes 4194304 | tf_op jit(solution)/shard_map/psum | solution.py:195
  539.8 22.1 %copy-start.9 = (bf16[128,128]{0,1:T(8,128)(2,1)S(1)}, bf16[128,128]{0,1:T(8,128)(2,1)}, u32[]{:S(2)}) copy-start(bf16[128,128]{0,1:T(8,128)(2,1)} %reduce-scatter.7.cloned.1.call-done) | copy-start | bytes 98308
  556.9 5.0 copy-start.10
  561.9 110.5 %all-gather.15.cloned.1.call-start = ((), (), s32[]{:S(2)}) async-start(), calls=%async_computation.14 | async-start | bytes 2949120 | tf_op jit(solution)/shard_map/all_gather | solution.py:207
  562.7 8.0 %copy-start.11 = (bf16[2048]{0:T(1024)(128)(2,1)S(1)}, bf16[2048]{0:T(1024)(128)(2,1)}, u32[]{:S(2)}) copy-start(bf16[2048]{0:T(1024)(128)(2,1)} %param.7) | copy-start | bytes 12292
  565.2 111.6 %all-to-all-start = ((bf16[128,8,1024]{0,2,1:T(8,128)(2,1)}), bf16[128,8,1024]{0,2,1:T(8,128)(2,1)}, u32[]{:S(2)}, u32[]{:S(2)}) async-start(bf16[128,8,1024]{0,2,1:T(8,128)(2,1)} %bitcast.166), calls=%async_computation.4 | async-start | bytes 4194304 | tf_op jit(solution)/shard_map/all_to_all | solution.py:206
  570.7 44.9 %copy-start = (bf16[128,8192]{1,0:T(8,128)(2,1)S(1)}, bf16[128,8192]{1,0:T(8,128)(2,1)}, u32[]{:S(2)}) copy-start(bf16[128,8192]{1,0:T(8,128)(2,1)} %all-gather.7.cloned.1.call-done) | copy-start | bytes 6291460
  570.7 45.7 %copy-start.3 = (bf16[128,2048]{1,0:T(8,128)(2,1)S(1)}, bf16[128,2048]{1,0:T(8,128)(2,1)}, u32[]{:S(2)}) copy-start(bf16[128,2048]{1,0:T(8,128)(2,1)} %param.6) | copy-start | bytes 1572868
  613.4 2.2 copy-start.2
Sparse Core Ops, SparseCore 0:
  9.5 25.2 all-gather.6
  37.0 49.0 all-gather.12
  88.2 47.6 all-gather.8
  137.9 230.0 all-gather.10
  387.2 60.2 reduce-scatter.4
  451.3 61.1 reduce-scatter.8
  515.5 18.7 reduce-scatter.6
  537.2 19.6 reduce-scatter.10
  562.0 51.3 all-reduce.1
  615.9 56.4 all-gather.14
where the time goes:
time: 711 us; the launch traced here: 710 us
  waiting for transfers between devices  478 us (67%)
  blocking collectives  108 us (15%)
  matrix products  60.2 us (8%)
  other arithmetic  24.1 us (3%)
  local copies, waits for them, and re-layouts  19.3 us (3%)
  between operations  14.6 us (2%)
    all_gather x1, waiting for transfers between devices, on_device(): lax.all_gather(w_query, 'dp', axis=0, tiled=True)  156 us
    reduce_scatter x1, waiting for transfers between devices, on_device(): lax.psum_scatter(dkey_part.reshape(seq_length, own_kv * head_width).astyp...  56.3 us
    reduce_scatter x1, waiting for transfers between devices, on_device(): lax.psum_scatter(dvalue_part.reshape(seq_length, own_kv * head_width).ast...  47.7 us
    all_gather x1, waiting for transfers between devices, on_device(): lax.all_gather(w_value, 'dp', axis=0, tiled=True)  47 us
    psum x1, waiting for transfers between devices, on_device(): lax.psum(partial_input.astype(jnp.bfloat16), 'tensor').astype(jnp.float32)  42.7 us
    all_gather x1, waiting for transfers between devices, on_device(): lax.all_gather(w_key, 'dp', axis=0, tiled=True)  41.7 us
    all_gather x1, blocking collectives, on_device(): lax.all_gather(value_half, 'dp', axis=0, tiled=True)  34.9 us
    all_gather x1, blocking collectives, on_device(): lax.all_gather(key_rot, 'dp', axis=0, tiled=True)  32.5 us
  transfers between devices with their start and end apart: 11, of which 10 were waited for; matrix products, arithmetic and copies ran while one was open for 7% of the time, Pallas kernels for 0%

commit v1 on v0

v1 whole, which is shorter than its diff:
```python
import jax
import jax.numpy as jnp
from jax import lax
from jax.sharding import PartitionSpec as P

QHEADS = 32
KVHEADS = 4
HD = 128


EPS = 1e-05
THETA = 500000.0


def angles(positions, head_width):
    frequency = THETA ** (-(jnp.arange(head_width // 2, dtype=jnp.float32) * 2.0) / head_width)
    turned = positions.astype(jnp.float32)[:, None] * frequency[None, :]
    return (jnp.cos(turned)[:, None, :], jnp.sin(turned)[:, None, :])


def rotate(field, cosine_table, sine_table):
    half_width = field.shape[-1] // 2
    front_half = field[..., :half_width]
    back_half = field[..., half_width:]
    return jnp.concatenate(
        [
            front_half * cosine_table - back_half * sine_table,
            back_half * cosine_table + front_half * sine_table,
        ],
        -1,
    )


def rotate_back(field, cosine_table, sine_table):
    half_width = field.shape[-1] // 2
    front_half = field[..., :half_width]
    back_half = field[..., half_width:]
    return jnp.concatenate(
        [
            front_half * cosine_table + back_half * sine_table,
            back_half * cosine_table - front_half * sine_table,
        ],
        -1,
    )


def head_major(columns, kv_total):
    count = columns // kv_total
    source = jnp.arange(columns, dtype=jnp.int32)
    target = (source % kv_total) * count + source // kv_total
    return (target[:, None] == source[None, :]).astype(jnp.bfloat16)


def dot32(left, right):
    return jnp.dot(left, right, preferred_element_type=jnp.float32)


def spread(field, axis, size):
    copies = jnp.broadcast_to(field[None], (size,) + field.shape)
    return lax.all_to_all(copies, axis, 0, 0, tiled=True)


def make(n_dp, n_tensor):
    n_core = 2 if n_tensor % 2 == 0 else 1
    n_chip = n_tensor // n_core

    def to_core(field):
        return lax.ppermute(field, "tensor", [(m, m ^ 1) for m in range(n_tensor)])

    def to_chip(field, step):
        return lax.ppermute(
            field,
            "tensor",
            [(m, ((m // n_core + step) % n_chip) * n_core + m % n_core) for m in range(n_tensor)],
        )

    def on_device(checkpoint, norm_gain, w_query, w_key, w_value, grad_attn):
        tokens, slice_width = checkpoint.shape
        few = tokens // n_tensor
        width = slice_width * n_tensor
        rows, query_cols = w_query.shape
        kv_cols = w_key.shape[1]
        kv_total = kv_cols * n_tensor // HD
        count = kv_cols // kv_total
        group_size = QHEADS // KVHEADS
        q_heads = query_cols // HD
        own_kv = max(1, q_heads // group_size)
        run_heads = q_heads // own_kv
        seq_length = tokens * n_dp

        def heads_of(member):
            first = member * q_heads // group_size
            return range(first, first + own_kv)

        x_rows = lax.all_to_all(checkpoint, "tensor", 0, 1, tiled=True)
        gain = spread(norm_gain, "tensor", n_tensor).reshape(width).astype(jnp.float32)
        x_wide = x_rows.astype(jnp.float32)
        inverse = lax.rsqrt(jnp.mean(x_wide * x_wide, -1, keepdims=True) + EPS)
        normed = (x_wide * inverse * gain).astype(jnp.bfloat16)
        own_cols = lax.all_to_all(normed, "dp", 1, 0, tiled=True).reshape(n_dp, few, rows)
        member = lax.axis_index("tensor")
        chip, core = member // n_core, member % n_core
        arrived = [(chip, own_cols)]
        for step in range(1, n_chip):
            arrived.append(((chip + n_chip - step) % n_chip, to_chip(own_cols, step)))
        features = jnp.zeros((n_dp, n_tensor, few, rows), jnp.bfloat16)
        for source, block in arrived:
            sides = [(core, block)]
            if n_core == 2:
                sides.append((1 - core, to_core(block)))
            for side, part in sides:
                features = lax.dynamic_update_slice_in_dim(
                    features, part[:, None], source * n_core + side, 1
                )
        features = features.reshape(seq_length, rows)

        order = head_major(kv_cols, kv_total)
        w_kv = jnp.concatenate(
            [dot32(w_key, order).astype(jnp.bfloat16), dot32(w_value, order).astype(jnp.bfloat16)],
            1,
        )

        def project(left, matrix):
            part = dot32(left, matrix).astype(jnp.bfloat16)
            return part.reshape(n_dp, tokens, matrix.shape[1])

        kv_part = project(features, w_kv)
        features, kv_part = lax.optimization_barrier((features, kv_part))
        kv_part = lax.all_to_all(kv_part, "dp", 0, 0, tiled=True)
        query_part = lax.all_to_all(project(features, w_query), "dp", 0, 0, tiled=True)
        kv_local = jnp.sum(kv_part.astype(jnp.float32), 0)
        key_local, value_local = kv_local[:, :kv_cols], kv_local[:, kv_cols:]
        queries = jnp.sum(query_part.astype(jnp.float32), 0).reshape(tokens, q_heads, HD)

        first_row = lax.axis_index("dp") * tokens
        own_positions = first_row + jnp.arange(tokens, dtype=jnp.int32)
        cosine_table, sine_table = angles(own_positions, HD)

        def for_member(other):
            pieces = [
                field[:, head * count : (head + 1) * count]
                for field in (key_local, value_local)
                for head in heads_of(other)
            ]
            return jnp.concatenate(pieces, 1)

        kv_send = jnp.stack([for_member(other) for other in range(n_tensor)])
        kv_got = lax.all_to_all(kv_send, "tensor", 0, 0, tiled=True)
        kv_heads = jnp.transpose(
            kv_got.reshape(n_tensor, tokens, 2 * own_kv, count), (1, 2, 0, 3)
        ).reshape(tokens, 2 * own_kv, HD)
        key_rot = rotate(kv_heads[:, :own_kv], cosine_table, sine_table)
        kv_half = jnp.concatenate([key_rot, kv_heads[:, own_kv:]], 1).astype(jnp.bfloat16)
        kv_all = spread(kv_half.reshape(tokens, 2 * own_kv * HD), "dp", n_dp)
        kv_all = kv_all.reshape(seq_length, 2 * own_kv, HD)
        keys_three = kv_all[:, :own_kv]
        values_three = kv_all[:, own_kv:]

        query_rot = rotate(queries, cosine_table, sine_table).astype(jnp.bfloat16)
        score_scale = HD ** (-0.5)
        query_grp = query_rot.reshape(tokens, own_kv, run_heads, HD)
        upstream = grad_attn.reshape(tokens, own_kv, run_heads, HD)
        scores = (
            jnp.einsum("tkgd,skd->kgts", query_grp, keys_three, preferred_element_type=jnp.float32)
            * score_scale
        )
        allowed = own_positions[:, None] >= jnp.arange(seq_length, dtype=jnp.int32)[None, :]
        scores = jnp.where(allowed, scores, -jnp.inf)
        row_top = jnp.max(scores, -1, keepdims=True)
        raw_weights = jnp.exp(scores - row_top)
        chances = raw_weights / jnp.sum(raw_weights, -1, keepdims=True)
        chances_half = chances.astype(jnp.bfloat16)
        attended = jnp.einsum(
            "kgts,skd->tkgd", chances_half, values_three, preferred_element_type=jnp.float32
        )
        row_delta = jnp.sum(upstream.astype(jnp.float32) * attended, -1)
        prob_grads = jnp.einsum(
            "tkgd,skd->kgts", upstream, values_three, preferred_element_type=jnp.float32
        )
        dscore = chances * (prob_grads - jnp.transpose(row_delta, (1, 2, 0))[..., None])
        dscore_half = dscore.astype(jnp.bfloat16)
        dkey_part = (
            jnp.einsum("kgts,tkgd->skd", dscore_half, query_grp, preferred_element_type=jnp.float32)
            * score_scale
        )
        dvalue_part = jnp.einsum(
            "kgts,tkgd->skd", chances_half, upstream, preferred_element_type=jnp.float32
        )
        dkv_part = jnp.concatenate([dkey_part, dvalue_part], 1).astype(jnp.bfloat16)
        dkv_part = lax.all_to_all(
            dkv_part.reshape(n_dp, tokens, 2 * own_kv * HD), "dp", 0, 0, tiled=True
        )
        dkv_sum = jnp.sum(dkv_part.astype(jnp.float32), 0).reshape(tokens, 2 * own_kv, HD)
        dquery = (
            jnp.einsum("kgts,skd->tkgd", dscore_half, keys_three, preferred_element_type=jnp.float32)
            * score_scale
        )
        dkey_back = rotate_back(dkv_sum[:, :own_kv], cosine_table, sine_table)
        dkv_back = jnp.concatenate([dkey_back, dkv_sum[:, own_kv:]], 1).astype(jnp.bfloat16)
        dkv_send = jnp.transpose(
            dkv_back.reshape(tokens, 2 * own_kv, n_tensor, count), (2, 0, 1, 3)
        ).reshape(n_tensor, tokens, 2 * own_kv * count)
        dkv_got = lax.all_to_all(dkv_send, "tensor", 0, 0, tiled=True)

        def own_columns(which):
            pieces = []
            for head in range(kv_total):
                found = []
                for member in range(n_tensor):
                    for place, held in enumerate(heads_of(member)):
                        if held == head:
                            at = (which * own_kv + place) * count
                            found.append(dkv_got[member, :, at : at + count])
                if len(found) == 1:
                    pieces.append(found[0])
                else:
                    pieces.append(sum(f.astype(jnp.float32) for f in found).astype(jnp.bfloat16))
            return jnp.concatenate(pieces, 1)

        dquery_pre = (
            rotate_back(dquery.reshape(tokens, q_heads, HD), cosine_table, sine_table)
            .astype(jnp.bfloat16)
            .reshape(tokens, query_cols)
        )
        piece_q = lax.all_gather(dquery_pre, "dp", axis=0, tiled=True)
        kv_grads = jnp.concatenate([own_columns(0), own_columns(1)], 1)
        piece_kv = spread(kv_grads, "dp", n_dp).reshape(seq_length, 2 * kv_cols)

        def side_of(side):
            def rows_of(field):
                split = field.reshape(n_dp, n_chip, n_core, few, field.shape[1])
                return lax.dynamic_index_in_dim(split, side, 2, keepdims=False).reshape(
                    n_dp * n_chip * few, field.shape[1]
                )

            total = jnp.einsum(
                "tc,dc->td", rows_of(piece_q), w_query, preferred_element_type=jnp.float32
            ) + jnp.einsum("tc,dc->td", rows_of(piece_kv), w_kv, preferred_element_type=jnp.float32)
            return total.astype(jnp.bfloat16).reshape(n_dp, n_chip, few, rows)

        if n_core == 2:
            theirs = to_core(side_of(1 - core))
            halves = side_of(core).astype(jnp.float32) + theirs.astype(jnp.float32)
        else:
            halves = side_of(core).astype(jnp.float32)
        dnormed = lax.dynamic_index_in_dim(halves, chip, 1, keepdims=False)
        for step in range(1, n_chip):
            block = lax.dynamic_index_in_dim(halves, (chip + step) % n_chip, 1, keepdims=False)
            dnormed = dnormed + to_chip(block.astype(jnp.bfloat16), step).astype(jnp.float32)
        dnormed = dnormed.astype(jnp.bfloat16)
        dnormed = lax.all_to_all(dnormed, "dp", 0, 1).reshape(few, width).astype(jnp.float32)
        row_sum = jnp.sum(gain * dnormed * x_wide, -1, keepdims=True)
        d_rows = (
            inverse * gain * dnormed - x_wide * inverse**3 * row_sum / width
        ).astype(jnp.bfloat16)
        d_checkpoint = lax.all_to_all(d_rows, "tensor", 1, 0, tiled=True)
        gain_part = jnp.sum(dnormed * x_wide * inverse, 0).reshape(n_tensor, slice_width)
        gain_part = jnp.sum(lax.all_to_all(gain_part, "tensor", 0, 0, tiled=True), 0)
        grad_gain = jnp.sum(spread(gain_part, "dp", n_dp), 0)

        def weight_grad(grads):
            return jnp.einsum("td,tc->dc", features, grads, preferred_element_type=jnp.float32)

        def storage_order(grads):
            return jnp.einsum(
                "tc,dc->td", grads, order, preferred_element_type=jnp.float32
            ).astype(jnp.bfloat16)

        grad_query = weight_grad(piece_q)
        grad_key = weight_grad(storage_order(piece_kv[:, :kv_cols]))
        grad_value = weight_grad(storage_order(piece_kv[:, kv_cols:]))
        return (d_checkpoint, grad_gain, grad_query, grad_key, grad_value)

    return on_device


def solution(mesh):
    return jax.shard_map(
        make(mesh.shape["dp"], mesh.shape["tensor"]),
        mesh=mesh,
        in_specs=(
            P(("sweep", "dp"), "tensor"),
            P(("sweep", "tensor")),
            P(("sweep", "dp"), "tensor"),
            P(("sweep", "dp"), "tensor"),
            P(("sweep", "dp"), "tensor"),
            P(("sweep", "dp"), "tensor"),
        ),
        out_specs=(
            P(("sweep", "dp"), "tensor"),
            P(("sweep", "tensor")),
            P(("sweep", "dp"), "tensor"),
            P(("sweep", "dp"), "tensor"),
            P(("sweep", "dp"), "tensor"),
        ),
        check_vma=False,
    )
```

time: 711 us -> 359 us (0.50)
  waiting for transfers between devices: 478 us -> 155 us
  blocking collectives: 108 us -> 34.3 us
  starting transfers between devices: 6.13 us -> 44.4 us
  local copies, waits for them, and re-layouts: 19.3 us -> 46.1 us
  matrix products: 60.2 us -> 36.2 us
    all_gather x5 -> x1, waiting for transfers between devices: 293 us -> 10.5 us  [on_device(): piece_q = lax.all_gather(dquery_pre, 'dp', axis=0, tiled=True)]
    reduce_scatter x4 -> x0, waiting for transfers between devices: 140 us -> none  [the longest x1 56.3 us: on_device(): lax.psum_scatter(dkey_part.reshape(seq_length, own_kv * head_width).astyp...]
    all_to_all x1 -> x11, waiting for transfers between devices: 0.01 us -> 120 us  [the longest x1 40.5 us: on_device(): lax.all_to_all(project(features, w_query), 'dp', 0, 0, tiled=True)]
    all_gather x5 -> x0, blocking collectives: 85 us -> none  [the longest x1 34.9 us: on_device(): lax.all_gather(value_half, 'dp', axis=0, tiled=True)]
    psum x1 -> x0, waiting for transfers between devices: 42.7 us -> none  [on_device(): lax.psum(partial_input.astype(jnp.bfloat16), 'tensor').astype(jnp.float32)]
    all_to_all x1 -> x11, starting transfers between devices: 5.51 us -> 43.6 us  [the longest x3 12.2 us: spread(): return lax.all_to_all(copies, axis, 0, 0, tiled=True)]
    all_to_all x0 -> x3, blocking collectives: none -> 34.3 us  [the longest x1 19.9 us: on_device(): lax.all_to_all(normed, 'dp', 1, 0, tiled=True).reshape(n_dp, few, rows)]
    ppermute x0 -> x5, waiting for transfers between devices: none -> 25.1 us  [the longest x2 25.1 us: to_chip(): lax.ppermute(field, 'tensor', [(m, (m // n_core + step) % n_chip * n_core...]
  transfers between devices with their start and end apart: 11 -> 17, of which waited for: 10 -> 13; matrix products, arithmetic and copies ran while one was open for 7% -> 15% of each run, Pallas kernels for 0% -> 0%
where the time goes in v1:
time: 359 us; the launch traced here: 357 us
  waiting for transfers between devices  155 us (43%)
  local copies, waits for them, and re-layouts  46.1 us (13%)
  starting transfers between devices  44.4 us (12%)
  matrix products  36.2 us (10%)
  blocking collectives  34.3 us (10%)
  other arithmetic  25.2 us (7%)
  between operations  14.8 us (4%)
    all_to_all x1, waiting for transfers between devices, on_device(): lax.all_to_all(project(features, w_query), 'dp', 0, 0, tiled=True)  40.5 us
    all_to_all x3, waiting for transfers between devices, spread(): return lax.all_to_all(copies, axis, 0, 0, tiled=True)  35.1 us
    ppermute x2, waiting for transfers between devices, to_chip(): lax.ppermute(field, 'tensor', [(m, (m // n_core + step) % n_chip * n_core...  25.1 us
    all_to_all x1, blocking collectives, on_device(): lax.all_to_all(normed, 'dp', 1, 0, tiled=True).reshape(n_dp, few, rows)  19.9 us
    all_to_all x1, waiting for transfers between devices, on_device(): kv_part = lax.all_to_all(kv_part, 'dp', 0, 0, tiled=True)  15.3 us
    dot_general x3, matrix products, weight_grad(): jnp.einsum('td,tc->dc', features, grads, preferred_element_type=jnp.float32)  13.5 us
    all_to_all x3, starting transfers between devices, spread(): return lax.all_to_all(copies, axis, 0, 0, tiled=True)  12.2 us
    all_gather x1, waiting for transfers between devices, on_device(): piece_q = lax.all_gather(dquery_pre, 'dp', axis=0, tiled=True)  10.5 us
  transfers between devices with their start and end apart: 17, of which 13 were waited for; matrix products, arithmetic and copies ran while one was open for 15% of the time, Pallas kernels for 0%

profile of v1, /device:TPU:0, one launch (start us, length us, event | category | flops | bytes accessed | tf_op | source)
XLA Modules:
  0.0 356.6 jit_solution(2678582230600630275)
XLA Ops:
  9.3 7.9 %all_to_all.107 = bf16[4,2,1024]{2,1,0:T(2,128)(2,1)S(1)} all-to-all(bf16[4,2,1024]{2,1,0:T(2,128)(2,1)S(1)} %reshape.461), channel_id=1, replica_groups=mesh['sweep'=1,'dp'=8,'tensor'=4] {'tensor'}, dimensions={0} | all-to-all | bytes 32768 | tf_op jit(solution)/shard_map/all_to_all | solution.py:60
  17.2 3.5 all-to-all-start
  20.9 8.6 %all-to-all-done = bf16[4,32,2048]{2,1,0:T(8,128)(2,1)S(1)} async-done(((bf16[4,32,2048]{2,1,0:T(8,128)(2,1)}), bf16[4,32,2048]{2,1,0:T(8,128)(2,1)S(1)}, u32[]{:S(2)}, u32[]{:S(2)}) %all-to-all-start) | async-done | bytes 524320 | tf_op jit(solution)/shard_map/all_to_all | solution.py:95
  34.2 19.9 %all_to_all.108 = bf16[32,8,1024]{2,0,1:T(8,128)(2,1)} all-to-all(bf16[32,8,1024]{2,0,1:T(8,128)(2,1)S(1)} %copy.178), channel_id=1, replica_groups=mesh['sweep'=1,'dp'=8,'tensor'=4] {'dp'}, dimensions={1} | all-to-all | bytes 1048576 | tf_op jit(solution)/shard_map/all_to_all | solution.py:100
  56.6 10.4 %collective-permute-done.1 = bf16[8,32,1024]{2,1,0:T(8,128)(2,1)} collective-permute-done((bf16[8,32,1024]{2,1,0:T(8,128)(2,1)}, bf16[8,32,1024]{2,1,0:T(8,128)(2,1)}, u32[]{:S(2)}, u32[]{:S(2)}) %collective-permute-start.1) | collective-permute-done | bytes 524320 | tf_op jit(solution)/shard_map/ppermute | solution.py:71
  72.2 4.3 %all-to-all-start.3 = ((bf16[8,128,256]{2,1,0:T(8,128)(2,1)}), bf16[8,128,256]{2,1,0:T(8,128)(2,1)}, u32[]{:S(2)}, u32[]{:S(2)}) async-start(bf16[8,128,256]{2,1,0:T(8,128)(2,1)} %bitcast.306), calls=%async_computation.3 | async-start | bytes 1048576 | tf_op jit(solution)/shard_map/all_to_all | solution.py:129
  76.5 15.3 %all-to-all-done.3 = bf16[8,128,256]{2,1,0:T(8,128)(2,1)} async-done(((bf16[8,128,256]{2,1,0:T(8,128)(2,1)}), bf16[8,128,256]{2,1,0:T(8,128)(2,1)}, u32[]{:S(2)}, u32[]{:S(2)}) %all-to-all-start.3) | async-done | bytes 524320 | tf_op jit(solution)/shard_map/all_to_all | solution.py:129
  95.7 3.3 all-to-all-start.4
  99.1 4.6 %all-to-all-done.4 = f32[4,128,64]{1,2,0:T(8,128)S(1)} async-done(((f32[4,128,64]{1,2,0:T(8,128)}), f32[4,128,64]{1,2,0:T(8,128)S(1)}, u32[]{:S(2)}, u32[]{:S(2)}) %all-to-all-start.4) | async-done | bytes 131104 | tf_op jit(solution)/shard_map/all_to_all | solution.py:148
  104.8 4.2 %all-to-all-start.5 = ((bf16[8,128,256]{1,2,0:T(8,128)(2,1)}), bf16[8,128,256]{1,2,0:T(8,128)(2,1)}, u32[]{:S(2)}, u32[]{:S(2)}) async-start(bf16[8,128,256]{1,2,0:T(8,128)(2,1)} %broadcast_in_dim.31), calls=%async_computation.5 | async-start | bytes 1048576 | tf_op jit(solution)/shard_map/all_to_all | solution.py:60
  108.9 5.2 %convolution_convert_fusion = bf16[1024,1024]{1,0:T(8,128)(2,1)} fusion(bf16[1024,1024]{1,0:T(8,128)(2,1)} %bitcast.287, bf16[1024,1024]{1,0:T(8,128)(2,1)S(1)} %copy-done), kind=kOutput, calls=%fused_computation.21 | convolution fusion | flops 2148532224 | bytes 6291456 | tf_op jit(solution)/shard_map/dot_general | solution.py:55
  114.2 9.1 %all-to-all-done.5 = bf16[8,128,256]{1,2,0:T(8,128)(2,1)} async-done(((bf16[8,128,256]{1,2,0:T(8,128)(2,1)}), bf16[8,128,256]{1,2,0:T(8,128)(2,1)}, u32[]{:S(2)}, u32[]{:S(2)}) %all-to-all-start.5) | async-done | bytes 524320 | tf_op jit(solution)/shard_map/all_to_all | solution.py:60
  123.3 4.5 %all-to-all-start.6 = ((bf16[8,128,1024]{2,1,0:T(8,128)(2,1)}), bf16[8,128,1024]{2,1,0:T(8,128)(2,1)}, u32[]{:S(2)}, u32[]{:S(2)}) async-start(bf16[8,128,1024]{2,1,0:T(8,128)(2,1)} %bitcast.294), calls=%async_computation.6 | async-start | bytes 4194304 | tf_op jit(solution)/shard_map/all_to_all | solution.py:130
  135.0 40.5 %all-to-all-done.6 = bf16[8,128,1024]{2,1,0:T(8,128)(2,1)} async-done(((bf16[8,128,1024]{2,1,0:T(8,128)(2,1)}), bf16[8,128,1024]{2,1,0:T(8,128)(2,1)}, u32[]{:S(2)}, u32[]{:S(2)}) %all-to-all-start.6) | async-done | bytes 2097184 | tf_op jit(solution)/shard_map/all_to_all | solution.py:130
  175.6 2.8 convert_reduce_fusion
  196.7 4.3 %all-to-all-start.7 = ((bf16[8,128,256]{1,2,0:T(8,128)(2,1)}), bf16[8,128,256]{1,2,0:T(8,128)(2,1)}, u32[]{:S(2)}, u32[]{:S(2)}) async-start(bf16[8,128,256]{1,2,0:T(8,128)(2,1)} %copy.203), calls=%async_computation.7 | async-start | bytes 1048576 | tf_op jit(solution)/shard_map/all_to_all | solution.py:190
  206.6 8.6 %all-to-all-done.7 = bf16[8,128,256]{1,2,0:T(8,128)(2,1)} async-done(((bf16[8,128,256]{1,2,0:T(8,128)(2,1)}), bf16[8,128,256]{1,2,0:T(8,128)(2,1)}, u32[]{:S(2)}, u32[]{:S(2)}) %all-to-all-start.7) | async-done | bytes 524320 | tf_op jit(solution)/shard_map/all_to_all | solution.py:190
  216.6 6.5 %all_to_all.109 = bf16[4,128,64]{1,2,0:T(8,128)(2,1)S(1)} all-to-all(bf16[4,128,64]{1,2,0:T(8,128)(2,1)S(1)} %bitcast.313), channel_id=1, replica_groups=mesh['sweep'=1,'dp'=8,'tensor'=4] {'tensor'}, dimensions={0} | all-to-all | bytes 131072 | tf_op jit(solution)/shard_map/all_to_all | solution.py:203
  224.1 4.4 %all-to-all-start.9 = ((bf16[8,128,256]{2,1,0:T(8,128)(2,1)}), bf16[8,128,256]{2,1,0:T(8,128)(2,1)}, u32[]{:S(2)}, u32[]{:S(2)}) async-start(bf16[8,128,256]{2,1,0:T(8,128)(2,1)} %broadcast_in_dim.34), calls=%async_computation.9 | async-start | bytes 1048576 | tf_op jit(solution)/shard_map/all_to_all | solution.py:60
  228.5 21.8 %all-to-all-done.9 = bf16[8,128,256]{2,1,0:T(8,128)(2,1)} async-done(((bf16[8,128,256]{2,1,0:T(8,128)(2,1)}), bf16[8,128,256]{2,1,0:T(8,128)(2,1)}, u32[]{:S(2)}, u32[]{:S(2)}) %all-to-all-start.9) | async-done | bytes 524320 | tf_op jit(solution)/shard_map/all_to_all | solution.py:60
  252.1 10.5 %all-gather.2.cloned.1.call-done = bf16[1024,1024]{0,1:T(8,128)(2,1)} async-done(((bf16[128,1024]{0,1:T(8,128)(2,1)}), bf16[1024,1024]{0,1:T(8,128)(2,1)}) %all-gather.2.cloned.1.call-update) | async-done | bytes 2097168 | tf_op jit(solution)/shard_map/all_gather | solution.py:225
  262.6 3.9 %copy.198 = bf16[1024,1024]{1,0:T(8,128)(2,1)} copy(bf16[1024,1024]{0,1:T(8,128)(2,1)} %all-gather.2.cloned.1.call-done) | data formatting | bytes 4194304 | tf_op jit(solution)/shard_map/all_gather | solution.py:225
  279.0 14.6 %collective-permute-done.4 = bf16[8,32,1024]{2,1,0:T(8,128)(2,1)} collective-permute-done((bf16[8,32,1024]{2,1,0:T(8,128)(2,1)}, bf16[8,32,1024]{2,1,0:T(8,128)(2,1)}, u32[]{:S(2)}, u32[]{:S(2)}) %collective-permute-start.4) | collective-permute-done | bytes 524320 | tf_op jit(solution)/shard_map/ppermute | solution.py:71
  296.0 4.4 %all-to-all-start.10 = ((bf16[8,32,1,1024]{3,1,2,0:T(8,128)(2,1)}), bf16[8,32,1,1024]{3,1,2,0:T(8,128)(2,1)}, u32[]{:S(2)}, u32[]{:S(2)}) async-start(bf16[8,32,1,1024]{3,1,2,0:T(8,128)(2,1)} %fusion.62), calls=%async_computation.10 | async-start | bytes 1048576 | tf_op jit(solution)/shard_map/all_to_all | solution.py:251
  301.8 3.4 fusion.47
  305.2 3.5 fusion.48
  308.7 6.1 %all-to-all-done.10 = bf16[8,32,1,1024]{3,1,2,0:T(8,128)(2,1)} async-done(((bf16[8,32,1,1024]{3,1,2,0:T(8,128)(2,1)}), bf16[8,32,1,1024]{3,1,2,0:T(8,128)(2,1)}, u32[]{:S(2)}, u32[]{:S(2)}) %all-to-all-start.10) | async-done | bytes 524320 | tf_op jit(solution)/shard_map/all_to_all | solution.py:251
  317.1 3.3 all-to-all-start.12
  326.1 3.6 %all-to-all-start.13 = ((f32[8,1,2048]{2,1,0:T(1,128)}), f32[8,1,2048]{2,1,0:T(1,128)S(1)}, u32[]{:S(2)}, u32[]{:S(2)}) async-start(f32[8,1,2048]{2,1,0:T(1,128)} %broadcast_in_dim.36), calls=%async_computation.13 | async-start | bytes 131072 | tf_op jit(solution)/shard_map/all_to_all | solution.py:60
  332.5 4.2 %all-to-all-done.13 = f32[8,1,2048]{2,1,0:T(1,128)S(1)} async-done(((f32[8,1,2048]{2,1,0:T(1,128)}), f32[8,1,2048]{2,1,0:T(1,128)S(1)}, u32[]{:S(2)}, u32[]{:S(2)}) %all-to-all-start.13) | async-done | bytes 65568 | tf_op jit(solution)/shard_map/all_to_all | solution.py:60
  336.7 3.7 %all-to-all-start.11 = ((bf16[32,4,2048]{2,0,1:T(8,128)(2,1)}), bf16[32,4,2048]{2,0,1:T(8,128)(2,1)S(1)}, u32[]{:S(2)}, u32[]{:S(2)}) async-start(bf16[32,4,2048]{2,0,1:T(8,128)(2,1)} %fusion.59), calls=%async_computation.11 | async-start | bytes 1048576 | tf_op jit(solution)/shard_map/all_to_all | solution.py:256
  340.4 6.6 %fusion.111 = f32[1024,1024]{1,0:T(8,128)} fusion(bf16[1024,1024]{1,0:T(8,128)(2,1)} %bitcast.290, bf16[1024,1024]{0,1:T(8,128)(2,1)} %all-gather.2.cloned.1.call-done), kind=kOutput, calls=%fused_computation.165 | convolution fusion | flops 2147483648 | bytes 8388608 | tf_op jit(solution)/shard_map/td,tc->dc/dot_general | solution.py:262
  (155 shorter events, 84.2 us)
Async XLA Ops:
  7.2 101.8 %copy-start = (bf16[1024,1024]{1,0:T(8,128)(2,1)S(1)}, bf16[1024,1024]{1,0:T(8,128)(2,1)}, u32[]{:S(2)}) copy-start(bf16[1024,1024]{1,0:T(8,128)(2,1)} %param.8) | copy-start | bytes 6291460
  17.2 12.3 %all-to-all-start = ((bf16[4,32,2048]{2,1,0:T(8,128)(2,1)}), bf16[4,32,2048]{2,1,0:T(8,128)(2,1)S(1)}, u32[]{:S(2)}, u32[]{:S(2)}) async-start(bf16[4,32,2048]{2,1,0:T(8,128)(2,1)} %bitcast.305), calls=%async_computation | async-start | bytes 1048576 | tf_op jit(solution)/shard_map/all_to_all | solution.py:95
  20.7 9.5 %copy-start.18 = (bf16[4,1,2048]{2,1,0:T(2,128)(2,1)}, bf16[4,1,2048]{2,1,0:T(2,128)(2,1)S(1)}, u32[]{:S(2)}) copy-start(bf16[4,1,2048]{2,1,0:T(2,128)(2,1)S(1)} %reshape.462) | copy-start | bytes 49156
  20.8 34.0 %copy-start.16 = (f32[8,1024]{1,0:T(8,128)}, f32[8,1024]{1,0:T(8,128)S(1)}, u32[]{:S(2)}) copy-start(f32[8,1024]{1,0:T(8,128)S(1)} %reshape.447) | copy-start | bytes 98308
  32.4 22.5 %copy-start.21 = (bf16[1024,128]{1,0:T(8,128)(2,1)S(1)}, bf16[1024,128]{1,0:T(8,128)(2,1)}, u32[]{:S(2)}) copy-start(bf16[1024,128]{1,0:T(8,128)(2,1)} %param.9) | copy-start | bytes 786436
  54.1 12.9 %collective-permute-start.1 = (bf16[8,32,1024]{2,1,0:T(8,128)(2,1)}, bf16[8,32,1024]{2,1,0:T(8,128)(2,1)}, u32[]{:S(2)}, u32[]{:S(2)}) collective-permute-start(bf16[8,32,1024]{2,1,0:T(8,128)(2,1)} %bitcast.2), channel_id=1, source_target_pairs={{0,2},{1,3},{2,0},{3,1},{4,6},{5,7},{6,4},{7,5},{8,10},{9,11},{10,... | collective-permute-start | bytes 1572872 | tf_op jit(solution)/shard_map/ppermute | solution.py:71
  54.9 13.5 %collective-permute-start = (bf16[8,32,1024]{2,1,0:T(8,128)(2,1)}, bf16[8,32,1024]{2,1,0:T(8,128)(2,1)}, u32[]{:S(2)}, u32[]{:S(2)}) collective-permute-start(bf16[8,32,1024]{2,1,0:T(8,128)(2,1)} %bitcast.2), channel_id=1, source_target_pairs={{0,1},{1,0},{2,3},{3,2},{4,5},{5,4},{6,7},{7,6},{8,9},{9,8},{10,11... | collective-permute-start | bytes 1572872 | tf_op jit(solution)/shard_map/ppermute | solution.py:68
  56.6 14.1 %copy-start.7 = (bf16[1024,128]{0,1:T(8,128)(2,1)}, bf16[1024,128]{0,1:T(8,128)(2,1)S(1)}, u32[]{:S(2)}) copy-start(bf16[1024,128]{0,1:T(8,128)(2,1)S(1)} %fusion.53) | copy-start | bytes 786436
  67.0 3.6 collective-permute-start.2
  70.6 1.6 copy-start.1
  72.2 19.6 %all-to-all-start.3 = ((bf16[8,128,256]{2,1,0:T(8,128)(2,1)}), bf16[8,128,256]{2,1,0:T(8,128)(2,1)}, u32[]{:S(2)}, u32[]{:S(2)}) async-start(bf16[8,128,256]{2,1,0:T(8,128)(2,1)} %bitcast.306), calls=%async_computation.3 | async-start | bytes 1048576 | tf_op jit(solution)/shard_map/all_to_all | solution.py:129
  95.7 7.9 %all-to-all-start.4 = ((f32[4,128,64]{1,2,0:T(8,128)}), f32[4,128,64]{1,2,0:T(8,128)S(1)}, u32[]{:S(2)}, u32[]{:S(2)}) async-start(f32[4,128,64]{1,2,0:T(8,128)} %copy.182), calls=%async_computation.4 | async-start | bytes 262144 | tf_op jit(solution)/shard_map/all_to_all | solution.py:148
  104.8 18.6 %all-to-all-start.5 = ((bf16[8,128,256]{1,2,0:T(8,128)(2,1)}), bf16[8,128,256]{1,2,0:T(8,128)(2,1)}, u32[]{:S(2)}, u32[]{:S(2)}) async-start(bf16[8,128,256]{1,2,0:T(8,128)(2,1)} %broadcast_in_dim.31), calls=%async_computation.5 | async-start | bytes 1048576 | tf_op jit(solution)/shard_map/all_to_all | solution.py:60
  123.3 52.2 %all-to-all-start.6 = ((bf16[8,128,1024]{2,1,0:T(8,128)(2,1)}), bf16[8,128,1024]{2,1,0:T(8,128)(2,1)}, u32[]{:S(2)}, u32[]{:S(2)}) async-start(bf16[8,128,1024]{2,1,0:T(8,128)(2,1)} %bitcast.294), calls=%async_computation.6 | async-start | bytes 4194304 | tf_op jit(solution)/shard_map/all_to_all | solution.py:130
  196.7 7.0 %copy-start.13 = (f32[128,64]{1,0:T(8,128)S(1)}, f32[128,64]{1,0:T(8,128)}, u32[]{:S(2)}) copy-start(f32[128,64]{1,0:T(8,128)} %get-tuple-element.33) | copy-start | bytes 98308
  196.7 7.0 %copy-start.14 = (f32[128,64]{1,0:T(8,128)S(1)}, f32[128,64]{1,0:T(8,128)}, u32[]{:S(2)}) copy-start(f32[128,64]{1,0:T(8,128)} %get-tuple-element.34) | copy-start | bytes 98308
  196.7 18.5 %all-to-all-start.7 = ((bf16[8,128,256]{1,2,0:T(8,128)(2,1)}), bf16[8,128,256]{1,2,0:T(8,128)(2,1)}, u32[]{:S(2)}, u32[]{:S(2)}) async-start(bf16[8,128,256]{1,2,0:T(8,128)(2,1)} %copy.203), calls=%async_computation.7 | async-start | bytes 1048576 | tf_op jit(solution)/shard_map/all_to_all | solution.py:190
  201.0 61.7 %all-gather.2.cloned.1.call-start = ((), (), s32[]{:S(2)}) async-start(), calls=%async_computation.14 | async-start | bytes 2359296 | tf_op jit(solution)/shard_map/all_gather | solution.py:225
  224.1 26.2 %all-to-all-start.9 = ((bf16[8,128,256]{2,1,0:T(8,128)(2,1)}), bf16[8,128,256]{2,1,0:T(8,128)(2,1)}, u32[]{:S(2)}, u32[]{:S(2)}) async-start(bf16[8,128,256]{2,1,0:T(8,128)(2,1)} %broadcast_in_dim.34), calls=%async_computation.9 | async-start | bytes 1048576 | tf_op jit(solution)/shard_map/all_to_all | solution.py:60
  272.1 3.1 collective-permute-start.3
  272.1 2.6 copy-start.9
  272.1 2.6 copy-start.11
  278.1 22.3 %copy-start.19 = (bf16[4,1,2048]{2,1,0:T(2,128)(2,1)S(1)}, bf16[4,1,2048]{2,1,0:T(2,128)(2,1)}, u32[]{:S(2)}) copy-start(bf16[4,1,2048]{2,1,0:T(2,128)(2,1)} %copy-done.18) | copy-start | bytes 49156
  279.0 14.7 %collective-permute-start.4 = (bf16[8,32,1024]{2,1,0:T(8,128)(2,1)}, bf16[8,32,1024]{2,1,0:T(8,128)(2,1)}, u32[]{:S(2)}, u32[]{:S(2)}) collective-permute-start(bf16[8,32,1024]{2,1,0:T(8,128)(2,1)} %fusion.61), channel_id=1, source_target_pairs={{0,2},{1,3},{2,0},{3,1},{4,6},{5,7},{6,4},{7,5},{8,10},{9,11},{10,... | collective-permute-start | bytes 1572872 | tf_op jit(solution)/shard_map/ppermute | solution.py:71
  296.0 18.8 %all-to-all-start.10 = ((bf16[8,32,1,1024]{3,1,2,0:T(8,128)(2,1)}), bf16[8,32,1,1024]{3,1,2,0:T(8,128)(2,1)}, u32[]{:S(2)}, u32[]{:S(2)}) async-start(bf16[8,32,1,1024]{3,1,2,0:T(8,128)(2,1)} %fusion.62), calls=%async_computation.10 | async-start | bytes 1048576 | tf_op jit(solution)/shard_map/all_to_all | solution.py:251
  305.2 9.6 %copy-start.6 = (f32[1,32,8,1,1024]{4,2,1,3,0:T(8,128)S(1)}, f32[1,32,8,1,1024]{4,2,1,3,0:T(8,128)}, u32[]{:S(2)}) copy-start(f32[1,32,8,1,1024]{4,2,1,3,0:T(8,128)} %reshape.451) | copy-start | bytes 3145732
  305.2 9.6 %copy-start.17 = (f32[8,1024]{1,0:T(8,128)S(1)}, f32[8,1024]{1,0:T(8,128)}, u32[]{:S(2)}) copy-start(f32[8,1024]{1,0:T(8,128)} %copy-done.16) | copy-start | bytes 98308
  316.4 13.4 %copy-start.4 = (bf16[4,32,2048]{2,1,0:T(8,128)(2,1)S(1)}, bf16[4,32,2048]{2,1,0:T(8,128)(2,1)}, u32[]{:S(2)}) copy-start(bf16[4,32,2048]{2,1,0:T(8,128)(2,1)} %copy-done.3) | copy-start | bytes 1572868
  316.4 13.4 %copy-start.22 = (f32[32]{0:T(128)S(1)}, f32[32]{0:T(128)}, u32[]{:S(2)}) copy-start(f32[32]{0:T(128)} %get-tuple-element.35) | copy-start | bytes 388
  317.1 8.3 %all-to-all-start.12 = ((f32[4,1,2048]{2,1,0:T(1,128)}), f32[4,1,2048]{2,1,0:T(1,128)S(1)}, u32[]{:S(2)}, u32[]{:S(2)}) async-start(f32[4,1,2048]{2,1,0:T(1,128)} %all_to_all.90), calls=%async_computation.12 | async-start | bytes 65536 | tf_op jit(solution)/shard_map/all_to_all | solution.py:258
  326.1 10.5 %all-to-all-start.13 = ((f32[8,1,2048]{2,1,0:T(1,128)}), f32[8,1,2048]{2,1,0:T(1,128)S(1)}, u32[]{:S(2)}, u32[]{:S(2)}) async-start(f32[8,1,2048]{2,1,0:T(1,128)} %broadcast_in_dim.36), calls=%async_computation.13 | async-start | bytes 131072 | tf_op jit(solution)/shard_map/all_to_all | solution.py:60
  336.7 12.3 %all-to-all-start.11 = ((bf16[32,4,2048]{2,0,1:T(8,128)(2,1)}), bf16[32,4,2048]{2,0,1:T(8,128)(2,1)S(1)}, u32[]{:S(2)}, u32[]{:S(2)}) async-start(bf16[32,4,2048]{2,0,1:T(8,128)(2,1)} %fusion.59), calls=%async_computation.11 | async-start | bytes 1048576 | tf_op jit(solution)/shard_map/all_to_all | solution.py:256
  (8 other events, 9.7 us)
Sparse Core Ops, SparseCore 0:
  206.7 55.8 all-gather.1
